TPU v7x, 32 devices: a whole 2x2x4 slice. The times are simulated.
32 devices in a mesh: grp: 4 (over y, core), dev: 8 (over z, x).
Axes of the slice: x: 2, y: 2, z: 4, core: 2. Of those that a mesh axis runs over, the one named last changes fastest.
Arguments:
- old_fine: float32 [512, 9, 64, 128], P('dev', None, 'grp'), may hold values from -6 to 6
- old_ids: int32 [4, 512], P('grp', 'dev'), may hold values from -1 to 511, as said below
- old_coarse: float32 [256, 9, 32, 64], P('dev', None, 'grp'), may hold values from -6 to 6
- coarse_ids: int32 [4, 256], P('grp', 'dev'), may hold values from 0 to 255, as said below
- velocity: float32 [512, 3, 64, 128], P('dev', None, 'grp'), may hold values from -0.12 to 0.12
- diffusion: float32 [9], replicated, may hold values from 0.01 to 0.1
Outputs:
- species_out: float32 [512, 9, 64, 128], P('dev', None, 'grp')
Inputs may be any that keep to these rules, and one draw needn't show every extreme that they name: `old_ids`: row g names, for each old fine slot k of group g (on dev index k // 64), the x-plane that the slot holds, or -1 for an empty slot whose rows of old_fine are ignored. No plane is named twice; planes named nowhere are newly refined. The slots of one device hold at most 16 planes of any one new box, box e holding planes e * 64 to e * 64 + 63. `coarse_ids`: each row is a permutation. The slots of one device hold at most 8 of the coarse planes e * 32 to e * 32 + 31 of any one new box e.
All inputs are finite; a program needn't handle non-finite values.
Results may differ from a plain program's by a relative error of at most 0.000092.
Values sent between devices are 32-bit elements; how exact they have to be, the bound alone decides.
A program may use at most 192 MiB of HBM per device.

v0:
```python
import functools

import jax
import jax.numpy as jnp
from jax import lax
from jax.experimental import pallas as pl
from jax.experimental.pallas import tpu as pltpu
from jax.sharding import PartitionSpec as P

CROSS = (34, 36, 38, 40, 44)
FINE = (10, 11, 6, 6)
COARSE = (4, 2, 6, 6, 4)
VMEM_LIMIT = 48 * 1024 * 1024
MESH = pl.DeviceIdType.MESH


def params(**more):
    return pltpu.CompilerParams(vmem_limit_bytes=VMEM_LIMIT, **more)


def earlier_count(mask):
    count = mask.shape[-1]
    lower = jnp.arange(count)[None, :] < jnp.arange(count)[:, None]
    return jnp.sum((mask[..., None, :] & lower).astype(jnp.int32), axis=-1)


def send_table(labels, block_len, devices, capacity):
    target = jnp.where(labels >= 0, labels // block_len, -1)
    count = labels.shape[0]
    same = target[None, :] == target[:, None]
    lower = jnp.arange(count)[None, :] < jnp.arange(count)[:, None]
    rank = jnp.sum((same & lower).astype(jnp.int32), axis=1)
    slot = jnp.where(labels >= 0, target * capacity + rank, -1)
    hits = slot[None, :] == jnp.arange(devices * capacity)[:, None]
    return jnp.max(jnp.where(hits, jnp.arange(count)[None, :], 0), axis=1)


def receive_table(labels_all, block_len, capacity, me):
    devices, count = labels_all.shape
    within = labels_all - me * block_len
    valid = (within >= 0) & (within < block_len)
    slot = jnp.arange(devices)[:, None] * capacity + earlier_count(valid)
    flat_within = jnp.where(valid, within, -1).reshape(-1)
    hits = flat_within[None, :] == jnp.arange(block_len)[:, None]
    return jnp.max(jnp.where(hits, slot.reshape(-1)[None, :], -1), axis=1)


def same_dim(a, b, exact=None):
    return lax.dot_general(
        a, b, (((1,), (1,)), ((), ())), precision=exact,
        preferred_element_type=jnp.float32,
    )


def plain_dot(a, b):
    return jnp.dot(a, b, preferred_element_type=jnp.float32)


def as_float(mask):
    return jnp.where(mask, 1.0, 0.0)


def stacked(masks, right):
    out = plain_dot(jnp.concatenate(masks, axis=0), right)
    size = masks[0].shape[0]
    return [out[i * size : (i + 1) * size] for i in range(len(masks))]


def route(owner, devices, base, extra, step, inner, stride, depth, hops):
    shape = owner.shape
    rows, count = shape
    part = devices // 2
    src = lax.rem(lax.broadcasted_iota(jnp.int32, shape, 0), devices)
    home, spot0 = src // part, lax.rem(src, part)
    first = lax.broadcasted_iota(jnp.int32, (count, count), 0)
    second = lax.broadcasted_iota(jnp.int32, (count, count), 1)
    before = as_float(first < second)
    ones = jnp.ones((count, count), jnp.float32)
    masks = [as_float(owner == e) for e in range(devices)]
    ranks = stacked(masks, before)
    counts = [c.astype(jnp.int32) for c in stacked(masks, ones)]
    rank = sum(m * r for m, r in zip(masks, ranks)).astype(jnp.int32)
    caps = []
    for v in range(devices):
        turn = lax.rem(v + part - spot0, part)
        wide = base + jnp.where(turn < extra, step, 0)
        caps.append(jnp.where(home != v // part, wide, inner))
    limit = sum(jnp.where(owner == v, caps[v], 0) for v in range(devices))
    valid = owner >= 0
    over = valid & (rank >= limit)
    side = jnp.where(valid, owner // part, -1)
    orders = stacked([as_float(over & (side == h)) for h in range(2)], before)
    order = jnp.where(side == 0, orders[0], orders[1]).astype(jnp.int32)
    lent_via = jnp.full(shape, -1, jnp.int32)
    lent_spot = jnp.zeros(shape, jnp.int32)
    for h in range(2):
        passed = jnp.zeros(shape, jnp.int32)
        seek = jnp.where(over & (side == h), order, -1)
        for l in range(stride - 1, -1, -1):
            for v in range(h * part, (h + 1) * part):
                free = (counts[v] <= l) & (caps[v] > l)
                hit = free & (seek == passed)
                lent_via = jnp.where(hit, v, lent_via)
                lent_spot = jnp.where(hit, l, lent_spot)
                passed = passed + jnp.where(free, 1, 0)
    via = jnp.where(over, lent_via, owner)
    spot = jnp.where(over, lent_spot, rank)
    relayed = over & (via >= 0) & (via != owner)
    limit_via = sum(jnp.where(via == v, caps[v], 0) for v in range(devices))
    deep = relayed & (spot < limit_via - depth)
    bad = (over & (lent_via < 0)) | deep
    lanes = [
        (v, e) for v in range(devices) for e in range(devices)
        if v != e and v // part == e // part
    ]
    hops_at = [as_float(relayed & (via == v) & (owner == e)) for v, e in lanes]
    inside = stacked(hops_at, before)
    total = stacked(hops_at, jnp.ones((count, 128), jnp.float32))
    lane = lax.broadcasted_iota(jnp.int32, (rows, 128), 1)
    table = sum(jnp.where(lane == i, t, 0.0) for i, t in enumerate(total))
    up = lax.broadcasted_iota(jnp.int32, (rows, rows), 0)
    across = lax.broadcasted_iota(jnp.int32, (rows, rows), 1)
    earlier = as_float((up // devices == across // devices) & (across < up))
    ahead = plain_dot(earlier, table)
    index = jnp.zeros(shape, jnp.float32)
    for i, m in enumerate(hops_at):
        index = index + m * (inside[i] + ahead[:, i : i + 1])
    crowded = jnp.max(ahead + table, axis=(0, 1), keepdims=True) > hops
    fault = jnp.max(as_float(bad), axis=(0, 1), keepdims=True) > 0.0
    return via, spot, relayed, index.astype(jnp.int32), caps, crowded | fault


def widest_load(owner, devices):
    part = devices // 2
    src = lax.rem(lax.broadcasted_iota(jnp.int32, owner.shape, 0), devices)
    away = (owner >= 0) & (owner // part != src // part)
    load = jnp.sum(as_float(away), axis=1, keepdims=True)
    return jnp.max(load, axis=0, keepdims=True)


def plan_kernel(
    groups, devices, block_len, coarse_len, sizes, choices,
    place, fine_ids, coarse_ids, out, via_ref, where_ref, kind_ref, owner_ref, inner_ref,
):
    inner, stride, depth, hops, base_c, extra_c, step_c, inner_c, stride_c, hops_c = sizes
    part = devices // 2
    g, me = place[0], place[1]
    fine, coarse = fine_ids[...], coarse_ids[...]
    rows, count = fine.shape
    count_c = coarse.shape[1]
    width = out.shape[1]
    owner = jnp.where(fine >= 0, fine // block_len, -1)
    load = widest_load(owner, devices)
    pick = sum(jnp.where(load > float(c), 1, 0) for c in choices)
    wide = sum(jnp.where(pick == i, c, 0) for i, c in enumerate(choices))
    base, extra = wide // part, lax.rem(wide, part)

    both = jnp.where(fine >= 0, lax.rem(fine, block_len) // 2, -1)
    kind = lax.broadcasted_iota(jnp.int32, (devices, count), 0)
    cell = lax.broadcasted_iota(jnp.int32, (coarse_len, count), 0)
    cell_c = lax.broadcasted_iota(jnp.int32, (coarse_len, count_c), 0)
    kind_c = lax.broadcasted_iota(jnp.int32, (devices, count_c), 0)
    owner_c = coarse // coarse_len
    within_c = lax.rem(coarse, coarse_len)
    needed = []
    for k in range(groups):
        held = jnp.zeros((devices, coarse_len), jnp.float32)
        for s in range(devices):
            r = k * devices + s
            held = held + same_dim(
                as_float(owner[r : r + 1] == kind), as_float(both[r : r + 1] == cell)
            )
        for s in range(devices):
            r = k * devices + s
            seen = plain_dot(held, as_float(within_c[r : r + 1] == cell_c))
            seen = jnp.where(owner_c[r : r + 1] == kind_c, seen, 0.0)
            needed.append(jnp.sum(seen, axis=0, keepdims=True))
    needed = jnp.concatenate(needed, axis=0) < 1.5
    owner_c = jnp.where(needed, owner_c, -1)

    def tables(owner, ids, length, stride, hops, depth, base, extra, step, inner, start):
        via, spot, relayed, index, caps, fault = route(
            owner, devices, base, extra, step, inner, stride, depth, hops
        )
        n = owner.shape[1]
        src = lax.rem(lax.broadcasted_iota(jnp.int32, owner.shape, 0), devices)
        turn = lax.rem(lax.rem(via, part) + part - lax.rem(src, part), part)
        block = jnp.where(via // part != src // part, turn, part + turn)
        cap = sum(jnp.where(via == v, caps[v], 0) for v in range(devices))
        late = stride - depth
        early = spot >= cap - depth
        flat = jnp.where(
            early, devices * late + block * depth + spot - (cap - depth), block * late + spot
        )
        flat = jnp.where(via >= 0, flat, -1)
        arrivals = devices * stride
        small = max(n, arrivals + (part - 1) * hops + 1) <= 256
        exact = None if small else lax.Precision.HIGHEST
        via_ref[:, 0:n] = jnp.where(relayed, via, -1)
        where_ref[:, 0:n] = flat
        kind_ref[:, 0:n] = index
        owner_ref[:, 0:n] = owner
        inner_ref[:, 0:n] = ids - me * length
        mine = pl.ds(pl.multiple_of(g * devices, devices), devices)
        via_g = via_ref[mine, 0:n]
        flat_g = where_ref[mine, 0:n]
        index_g = kind_ref[mine, 0:n]
        owner_g = owner_ref[mine, 0:n]
        inner_g = inner_ref[mine, 0:n]
        source = lax.broadcasted_iota(jnp.int32, (devices, n), 0)
        own = jnp.max(jnp.where(source == me, flat_g, -1), axis=0, keepdims=True)
        slots = lax.broadcasted_iota(jnp.int32, (width, n), 0)
        place_at = lax.broadcasted_iota(jnp.int32, (devices, n), 1).astype(jnp.float32)
        send = same_dim(place_at, as_float(own == slots), exact)
        lane = lax.rem(owner_g + 2 * part - lax.rem(me, part), part) - 1
        handed = jnp.where(via_g == me, lane * hops + index_g, -1)
        back = lax.rem(lax.rem(me, part) + part - lax.rem(jnp.maximum(via_g, 0), part), part) - 1
        spot_at = jnp.where(via_g >= 0, arrivals + back * hops + index_g, flat_g)
        inside = jnp.where(owner_g == me, inner_g, -1)
        flat_f = flat_g.astype(jnp.float32)
        spot_f = spot_at.astype(jnp.float32) + 1.0
        relay = jnp.zeros((devices, width), jnp.float32)
        final = jnp.zeros((devices, width), jnp.float32)
        for s in range(devices):
            relay = relay + same_dim(
                jnp.broadcast_to(flat_f[s : s + 1], (devices, n)),
                as_float(handed[s : s + 1] == slots), exact,
            )
            final = final + same_dim(
                jnp.broadcast_to(spot_f[s : s + 1], (devices, n)),
                as_float(inside[s : s + 1] == slots), exact,
            )
        at = lax.broadcasted_iota(jnp.int32, (devices, width), 1)
        whole = (final + 0.5).astype(jnp.int32)
        missing = start + (at // 2 if start else 0)
        whole = jnp.where(whole > 0, whole - 1, missing)
        send = (send + 0.5).astype(jnp.int32)
        relay = (relay + 0.5).astype(jnp.int32)
        return send, relay, whole, fault

    fill = devices * stride + (part - 1) * hops
    send, relay, final, fault = tables(
        owner, fine, block_len, stride, hops, depth, base, extra, 1, inner, fill
    )
    send_c, relay_c, final_c, fault_c = tables(
        owner_c, coarse, coarse_len, stride_c, hops_c, stride_c, base_c, extra_c, step_c, inner_c, 0
    )
    pick = jnp.where(fault | fault_c, len(choices), pick)
    parts = (send, relay, final, send_c, relay_c, final_c)
    for i, value in enumerate(parts):
        out[i : i + 1] = value[0:1]
    out[len(parts) : len(parts) + 1] = jnp.broadcast_to(pick, (1, width)).astype(jnp.int32)


def plan(place, fine_ids, coarse_ids, groups, devices, block_len, coarse_len, sizes, choices):
    rows, count = fine_ids.shape
    longest = max(devices * sizes[1], devices * sizes[8], count, (devices // 2) * max(sizes[3], sizes[9]))
    width = -(-longest // 128) * 128
    cells = pltpu.VMEM((rows, max(count, coarse_ids.shape[1])), jnp.int32)
    return pl.pallas_call(
        functools.partial(
            plan_kernel, groups, devices, block_len, coarse_len, sizes, choices
        ),
        out_shape=jax.ShapeDtypeStruct((8, width), jnp.int32),
        in_specs=[
            pl.BlockSpec(memory_space=pltpu.SMEM),
            pl.BlockSpec(memory_space=pltpu.VMEM),
            pl.BlockSpec(memory_space=pltpu.VMEM),
        ],
        out_specs=pl.BlockSpec(memory_space=pltpu.VMEM),
        scratch_shapes=[cells] * 5,
        compiler_params=params(),
        name="plan",
    )(place, fine_ids, coarse_ids)


def pack_fine_kernel(table, source, out, sem):
    def send(i, carry):
        pltpu.make_async_copy(source.at[table[i]], out.at[i], sem).start()
        return carry

    lax.fori_loop(0, out.shape[0], send, 0)
    pltpu.make_async_copy(out, out, sem).wait()


def pack_fine(table, fine):
    return pl.pallas_call(
        pack_fine_kernel,
        out_shape=jax.ShapeDtypeStruct((table.shape[0],) + fine.shape[1:], fine.dtype),
        in_specs=[
            pl.BlockSpec(memory_space=pltpu.SMEM),
            pl.BlockSpec(memory_space=pltpu.VMEM),
        ],
        out_specs=pl.BlockSpec(memory_space=pl.ANY),
        scratch_shapes=[pltpu.SemaphoreType.DMA],
        compiler_params=params(),
        name="pack_fine",
    )(table, fine)


def pack_coarse_kernel(table, source, out):
    half = source.shape[-1]

    def step(i, carry):
        out[i, :, :, 0:half] = source[table[2 * i]]
        out[i, :, :, half : 2 * half] = source[table[2 * i + 1]]
        return carry

    lax.fori_loop(0, out.shape[0], step, 0)


def pack_coarse(table, coarse):
    shape = (table.shape[0] // 2,) + coarse.shape[1:3] + (2 * coarse.shape[3],)
    return pl.pallas_call(
        pack_coarse_kernel,
        out_shape=jax.ShapeDtypeStruct(shape, coarse.dtype),
        in_specs=[
            pl.BlockSpec(memory_space=pltpu.SMEM),
            pl.BlockSpec(memory_space=pltpu.VMEM),
        ],
        out_specs=pl.BlockSpec(memory_space=pltpu.VMEM),
        compiler_params=params(),
        name="pack_coarse",
    )(table, coarse)


def refine_into(table, which, pairs, weights, out, offset, count):
    species, rows, depth = pairs.shape[1:]
    half = depth // 2
    lane = lax.broadcasted_iota(jnp.int32, (species * rows, depth), 1)
    row = lax.broadcasted_iota(jnp.int32, (species, rows, depth), 1)

    def step(c, carry):
        slot = jnp.maximum(table[which, c], 0)
        block = pairs[slot // 2].reshape(species * rows, depth)
        odd = slot % 2
        block = jnp.where((lane >= half).astype(jnp.int32) == odd, block, 0.0)
        spread = jnp.dot(
            block, weights[...], precision=lax.Precision.HIGHEST,
            preferred_element_type=jnp.float32,
        )
        plain = spread[:, :depth].reshape(species, rows, depth)
        sloped = spread[:, depth:].reshape(species, rows, depth)
        below = jnp.where(row == 0, plain, pltpu.roll(plain, 1, 1))
        above = jnp.where(row == rows - 1, plain, pltpu.roll(plain, rows - 1, 1))
        slope = 0.125 * (above - below)
        for s in range(species):
            out[offset + c, s, pl.ds(0, rows, 2), :] = sloped[s] - slope[s]
            out[offset + c, s, pl.ds(1, rows, 2), :] = sloped[s] + slope[s]
        return carry

    lax.fori_loop(0, count, step, 0)


def refine_kernel(table, pairs, weights, out):
    refine_into(table, 0, pairs, weights, out, 0, out.shape[0])


def spread_weights(half):
    depth = 2 * half
    coarse = jnp.arange(half)[:, None]
    fine = jnp.arange(depth)[None, :]
    centre = (fine // 2 == coarse).astype(jnp.float32)
    up = (jnp.minimum(fine // 2 + 1, half - 1) == coarse).astype(jnp.float32)
    down = (jnp.maximum(fine // 2 - 1, 0) == coarse).astype(jnp.float32)
    side = jnp.where(fine % 2 == 1, 0.125, -0.125)
    both = jnp.concatenate([centre, centre + side * (up - down)], axis=1)
    return jnp.concatenate([both, both], axis=0)


def refine(table, pairs, weights):
    species, rows, depth = pairs.shape[1:]
    return pl.pallas_call(
        refine_kernel,
        out_shape=jax.ShapeDtypeStruct(
            (table.shape[1], species, 2 * rows, depth), pairs.dtype
        ),
        in_specs=[
            pl.BlockSpec(memory_space=pltpu.SMEM),
            pl.BlockSpec(memory_space=pltpu.VMEM),
            pl.BlockSpec(memory_space=pltpu.VMEM),
        ],
        out_specs=pl.BlockSpec(memory_space=pltpu.VMEM),
        compiler_params=params(),
        cost_estimate=pl.CostEstimate(
            flops=40_000_000, bytes_accessed=30_000_000, transcendentals=0
        ),
        name="refine",
    )(table, pairs, weights)


def assemble_kernel(table, arrived, interp, out, sem):
    def fetch(p, carry):
        slot = table[p]

        @pl.when(slot >= 0)
        def _():
            pltpu.make_async_copy(arrived.at[slot], out.at[p], sem).start()

        @pl.when(slot < 0)
        def _():
            pltpu.make_async_copy(interp.at[p // 2], out.at[p], sem).start()

        return carry

    lax.fori_loop(0, out.shape[0], fetch, 0)
    pltpu.make_async_copy(out, out, sem).wait()


def assemble(table, arrived, interp):
    return pl.pallas_call(
        assemble_kernel,
        out_shape=jax.ShapeDtypeStruct((table.shape[0],) + arrived.shape[1:], arrived.dtype),
        in_specs=[
            pl.BlockSpec(memory_space=pltpu.SMEM),
            pl.BlockSpec(memory_space=pl.ANY),
            pl.BlockSpec(memory_space=pl.ANY),
        ],
        out_specs=pl.BlockSpec(memory_space=pltpu.VMEM),
        scratch_shapes=[pltpu.SemaphoreType.DMA],
        compiler_params=params(),
        name="assemble",
    )(table, arrived, interp)


def gather_kernel(groups, devices, mine, out, send_sems, recv_sems):
    total = groups * devices
    me = lax.axis_index("grp") * devices + lax.axis_index("dev")
    barrier = pltpu.get_barrier_semaphore()

    def place(k):
        to = lax.rem(me + k, total)
        return {"grp": to // devices, "dev": lax.rem(to, devices)}

    def greet(k, carry):
        pl.semaphore_signal(barrier, inc=1, device_id=place(k), device_id_type=MESH)
        return carry

    lax.fori_loop(1, total, greet, 0)
    pl.semaphore_wait(barrier, total - 1)

    def copy(k):
        return pltpu.make_async_remote_copy(
            src_ref=mine,
            dst_ref=out.at[me],
            send_sem=send_sems.at[k],
            recv_sem=recv_sems.at[k],
            device_id=place(k),
            device_id_type=MESH,
        )

    def start(k, carry):
        copy(k).start()
        return carry

    def finish(k, carry):
        copy(k).wait_send()
        source = lax.rem(me + total - k, total)
        pltpu.make_async_remote_copy(
            src_ref=mine,
            dst_ref=out.at[source],
            send_sem=send_sems.at[k],
            recv_sem=recv_sems.at[k],
            device_id=place(k),
            device_id_type=MESH,
        ).wait_recv()
        return carry

    lax.fori_loop(1, total, start, 0)
    out[me] = mine[...]
    lax.fori_loop(1, total, finish, 0)


def gather_ids(both, groups, devices):
    width = both.shape[0]
    padded = -(-width // 128) * 128
    mine = jnp.pad(both, (0, padded - width))[None]
    total = groups * devices
    out = pl.pallas_call(
        functools.partial(gather_kernel, groups, devices),
        out_shape=jax.ShapeDtypeStruct((total, 1, padded), both.dtype),
        in_specs=[pl.BlockSpec(memory_space=pltpu.VMEM)],
        out_specs=pl.BlockSpec(memory_space=pltpu.VMEM),
        scratch_shapes=[
            pltpu.SemaphoreType.DMA((total,)),
            pltpu.SemaphoreType.DMA((total,)),
        ],
        compiler_params=pltpu.CompilerParams(collective_id=0, has_side_effects=True),
        name="gather_ids",
    )(mine)
    return out.reshape(groups, devices, padded)[:, :, :width]


def coefficients(flow, x):
    v = [flow[x, k] for k in range(3)]
    plus = [jnp.maximum(w, 0.0) for w in v]
    minus = [jnp.maximum(-w, 0.0) for w in v]
    rest = 1.0
    for k in range(3):
        rest = rest - plus[k] - minus[k]
    return plus, minus, rest


def update(d, coeffs, c, lo, hi, below, above, row, lane):
    rows, depth = c.shape
    plus, minus, rest = coeffs
    ylo = jnp.where(row == 0, below, pltpu.roll(c, 1, 0))
    yhi = jnp.where(row == rows - 1, above, pltpu.roll(c, rows - 1, 0))
    zlo = jnp.where(lane == 0, c, pltpu.roll(c, 1, 1))
    zhi = jnp.where(lane == depth - 1, c, pltpu.roll(c, depth - 1, 1))
    total = (rest - 6.0 * d) * c
    total = total + (plus[0] + d) * lo + (minus[0] + d) * hi
    total = total + (plus[1] + d) * ylo + (minus[1] + d) * yhi
    return total + (plus[2] + d) * zlo + (minus[2] + d) * zhi


def regrid_kernel(
    cross, sizes, tables, diffusion, fine_hbm, coarse_hbm, weights, flow_hbm,
    out_hbm, first_out, last_out, below_out, above_out,
    fine, coarse, flow, out, load_sems, save_sems, send, send_c, pool, pool_c, near, handed, handed_c, passed_in, passed_c,
    state, low, high, below, above,
    low_next, high_next, below_next, above_next, first_next, last_next,
    send_sems, recv_sems, relay_send, relay_recv, edge_send, edge_recv, row_send, row_recv,
):
    inner, stride, depth, hops, base_c, extra_c, step_c, inner_c, stride_c, hops_c = sizes
    planes, species, rows, depth_z = fine.shape
    half_z = depth_z // 2
    groups, devices = lax.axis_size("grp"), lax.axis_size("dev")
    part = devices // 2
    late = stride - depth
    wide = [cross // part + (1 if k < cross % part else 0) for k in range(part)]
    wide_c = [base_c + (step_c if k < extra_c else 0) for k in range(part)]
    caps = wide + [inner] * part
    caps_c = wide_c + [inner_c] * part
    g, me = lax.axis_index("grp"), lax.axis_index("dev")
    base = (me // part) * part
    other = part - base
    seat = lax.rem(me, part)
    barrier = pltpu.get_barrier_semaphore()
    lane_c = lax.broadcasted_iota(jnp.int32, send_c.shape[1:], 2)

    def target(b):
        if b < part:
            return {"dev": other + lax.rem(seat + b, part)}
        return {"dev": base + lax.rem(seat + b - part, part)}

    def greet(to):
        pl.semaphore_signal(barrier, inc=1, device_id=to, device_id_type=MESH)

    loads = [
        pltpu.make_async_copy(source, into, load_sems.at[i])
        for i, (source, into) in enumerate(((fine_hbm, fine), (coarse_hbm, coarse), (flow_hbm, flow)))
    ]
    for load in loads:
        load.start()
    peers = list(range(part + 1, devices)) + list(range(part))
    for b in peers:
        greet(target(b))
    greet({"grp": lax.rem(g + 1, groups)})
    greet({"grp": lax.rem(g + groups - 1, groups)})
    pl.semaphore_wait(barrier, devices + 1)

    def remote(source, into, sems, at, to):
        return pltpu.make_async_remote_copy(
            src_ref=source,
            dst_ref=into,
            send_sem=sems[0].at[at],
            recv_sem=sems[1].at[at],
            device_id=to,
            device_id_type=MESH,
        )

    def pack(first, count, into, offset):
        def step(k, carry):
            into[offset + k] = fine[tables[0, first + k]]
            return carry

        lax.fori_loop(0, count, step, 0)

    def pack_coarse_pairs(first, count, into):
        def step(k, carry):
            into[first + k, :, :, 0:half_z] = coarse[tables[3, 2 * (first + k)]]
            into[first + k, :, :, half_z:depth_z] = coarse[tables[3, 2 * (first + k) + 1]]
            return carry

        lax.fori_loop(0, count, step, 0)

    sems = (send_sems, recv_sems)
    pairs_c = stride_c // 2
    coarse_moves, early_moves = [], []
    begin = devices * late
    near_by, far = peers[: part - 1], peers[part - 1 :]

    def send_coarse(b):
        count = caps_c[b] // 2
        first = b * pairs_c + pairs_c - count
        pack_coarse_pairs(first, count, send_c)
        cut = pl.ds(first, count)
        coarse_moves.append(remote(send_c.at[cut], pool_c.at[cut], sems, b, target(b)))
        coarse_moves[-1].start()

    def send_early(b):
        pack(begin + b * depth, depth, send, begin + b * depth)
        early_moves.append(
            remote(
                send.at[pl.ds(begin + b * depth, depth)], near.at[pl.ds(b * depth, depth)],
                sems, devices + b, target(b),
            )
        )
        early_moves[-1].start()

    def late_copy(b):
        cut = pl.ds(b * late, caps[b] - depth)
        return remote(send.at[cut], pool.at[cut], sems, 2 * devices + b, target(b))

    loads[0].wait()
    for b in far[:1]:
        send_early(b)
    loads[1].wait()
    for b in far:
        send_coarse(b)
    for b in far[1:]:
        send_early(b)
    for b in near_by:
        send_coarse(b)
        send_early(b)
        pack(b * late, inner - depth, send, b * late)
        late_copy(b).start()
    pack_coarse_pairs(part * pairs_c + pairs_c - inner_c // 2, inner_c // 2, pool_c)
    pack(begin + part * depth, depth, near, part * depth)
    pack(part * late, inner - depth, pool, part * late)
    for move in coarse_moves:
        move.wait_recv()

    def half_of(slot, odd):
        value = pool_c[slot // 2]
        turned = pltpu.roll(value, half_z, 2)
        return jnp.where(slot % 2 == odd, value, turned)

    def relay_coarse(k, carry):
        left = half_of(tables[4, 2 * k], 0)
        right = half_of(tables[4, 2 * k + 1], 1)
        handed_c[k] = jnp.where(lane_c < half_z, left, right)
        return carry

    sends_c = hops_c // 2
    relay_sems = (relay_send, relay_recv)
    lax.fori_loop(0, (part - 1) * sends_c, relay_coarse, 0)
    relays_c = []
    for k in range(1, part):
        cut = pl.ds((k - 1) * sends_c, sends_c)
        relays_c.append(remote(handed_c.at[cut], passed_c.at[cut], relay_sems, k, target(part + k)))
        relays_c[-1].start()
    for b in far:
        pack(b * late, caps[b] - depth, send, b * late)
    outer = (me < part // 2) | (me >= devices - part // 2)

    @pl.when(jnp.logical_not(outer))
    def _():
        for b in far:
            late_copy(b).start()

    for move in early_moves:
        move.wait_recv()

    passed = (part - 1) * hops

    def relay(k, carry):
        handed[k] = near[jnp.maximum(tables[1, k] - begin, 0)]
        return carry

    lax.fori_loop(0, passed, relay, 0)
    relays = []
    for k in range(1, part):
        cut = pl.ds((k - 1) * hops, hops)
        relays.append(
            remote(handed.at[cut], passed_in.at[cut], relay_sems, part + k, target(part + k))
        )
        relays[-1].start()

    @pl.when(outer)
    def _():
        for b in far:
            late_copy(b).start()

    late_moves = [late_copy(b) for b in peers]

    def keep_near(k, carry):
        pool[begin + k] = near[k]
        return carry

    lax.fori_loop(0, devices * depth, keep_near, 0)
    for move in relays_c:
        move.wait_recv()

    def keep_coarse(k, carry):
        pool_c[devices * pairs_c + k] = passed_c[k]
        return carry

    lax.fori_loop(0, (part - 1) * sends_c, keep_coarse, 0)
    arrivals = devices * stride
    refine_into(tables, 5, pool_c, weights, pool, arrivals + passed, coarse.shape[0])
    for move in late_moves + relays:
        move.wait_recv()

    def keep_passed(k, carry):
        pool[arrivals + k] = passed_in[k]
        return carry

    lax.fori_loop(0, passed, keep_passed, 0)

    def assemble(p, carry):
        at = tables[2, p]
        for s in range(species):
            value = pool[at, s]
            state[p + 1, s] = value
            low[s, pl.ds(p, 1), :] = value[0:1]
            high[s, pl.ds(p, 1), :] = value[rows - 1 : rows]
        return carry

    lax.fori_loop(0, planes, assemble, 0)

    def edge_copy(source, target, at, to):
        return pltpu.make_async_remote_copy(
            src_ref=source,
            dst_ref=target,
            send_sem=edge_send.at[at],
            recv_sem=edge_recv.at[at],
            device_id=to,
            device_id_type=MESH,
        )

    def row_copy(source, target, b, at, to):
        cut = pl.ds(pl.multiple_of(b * 8, 8), 8)
        return pltpu.make_async_remote_copy(
            src_ref=source.at[:, cut],
            dst_ref=target.at[:, cut],
            send_sem=row_send.at[at, b],
            recv_sem=row_recv.at[at, b],
            device_id=to,
            device_id_type=MESH,
        )

    left, right = {"dev": me - 1}, {"dev": me + 1}
    down, up = {"grp": g - 1}, {"grp": g + 1}
    ahead = edge_copy(state.at[pl.ds(planes, 1)], state.at[pl.ds(0, 1)], 0, right)
    back = edge_copy(state.at[pl.ds(1, 1)], state.at[pl.ds(planes + 1, 1)], 1, left)
    rise = edge_copy(high, below, 2, up)
    sink = edge_copy(low, above, 3, down)
    has_left, has_right = me > 0, me < devices - 1
    has_down, has_up = g > 0, g < groups - 1

    @pl.when(has_up)
    def _():
        rise.start()

    @pl.when(has_down)
    def _():
        sink.start()

    @pl.when(has_right)
    def _():
        ahead.start()

    @pl.when(has_left)
    def _():
        back.start()

    for move in coarse_moves + relays_c + early_moves + late_moves + relays:
        move.wait_send()

    @pl.when(has_left)
    def _():
        ahead.wait_recv()

    @pl.when(has_right)
    def _():
        back.wait_recv()

    @pl.when(has_down)
    def _():
        rise.wait_recv()

    @pl.when(has_up)
    def _():
        sink.wait_recv()

    @pl.when(has_right)
    def _():
        ahead.wait_send()

    @pl.when(has_left)
    def _():
        back.wait_send()

    @pl.when(has_up)
    def _():
        rise.wait_send()

    @pl.when(has_down)
    def _():
        sink.wait_send()

    @pl.when(me == 0)
    def _():
        state[0] = jnp.zeros(state.shape[1:], state.dtype)

    @pl.when(me == devices - 1)
    def _():
        state[planes + 1] = jnp.zeros(state.shape[1:], state.dtype)

    @pl.when(g == 0)
    def _():
        below[...] = jnp.zeros(below.shape, below.dtype)

    @pl.when(g == groups - 1)
    def _():
        above[...] = jnp.zeros(above.shape, above.dtype)

    row = lax.broadcasted_iota(jnp.int32, (rows, depth_z), 0)
    lane = lax.broadcasted_iota(jnp.int32, (rows, depth_z), 1)


    loads[2].wait()
    next_ahead = edge_copy(out.at[pl.ds(planes - 1, 1)], first_next, 4, right)
    next_back = edge_copy(out.at[pl.ds(0, 1)], last_next, 5, left)
    blocks = planes // 8

    def save(b):
        cut = pl.ds(b * 8, 8)
        return pltpu.make_async_copy(out.at[cut], out_hbm.at[cut], save_sems.at[b])

    def advance_block(turn, carry):
        b = lax.rem(turn + blocks - 1, blocks)

        def advance_plane(k, carry):
            p = b * 8 + k
            coeffs = coefficients(flow, p)
            for s in range(species):
                total = update(
                    diffusion[s], coeffs, state[p + 1, s], state[p, s], state[p + 2, s],
                    below[s, pl.ds(p, 1), :], above[s, pl.ds(p, 1), :], row, lane,
                )
                out[p, s] = total
                low_next[s, pl.ds(p, 1), :] = total[0:1]
                high_next[s, pl.ds(p, 1), :] = total[rows - 1 : rows]
            return carry

        lax.fori_loop(0, 8, advance_plane, 0)
        save(b).start()

        @pl.when(has_up)
        def _():
            row_copy(high_next, below_next, b, 0, up).start()

        @pl.when(has_down)
        def _():
            row_copy(low_next, above_next, b, 1, down).start()

        @pl.when((turn == 0) & has_right)
        def _():
            next_ahead.start()

        @pl.when((turn == 1) & has_left)
        def _():
            next_back.start()

        return carry

    lax.fori_loop(0, blocks, advance_block, 0)

    def settle(b, carry):
        save(b).wait()

        @pl.when(has_down)
        def _():
            row_copy(high_next, below_next, b, 0, up).wait_recv()
            row_copy(low_next, above_next, b, 1, down).wait_send()

        @pl.when(has_up)
        def _():
            row_copy(low_next, above_next, b, 1, down).wait_recv()
            row_copy(high_next, below_next, b, 0, up).wait_send()

        return carry

    lax.fori_loop(0, blocks, settle, 0)

    @pl.when(has_left)
    def _():
        next_ahead.wait_recv()
        next_back.wait_send()
        first_out[...] = first_next[...]

    @pl.when(has_right)
    def _():
        next_back.wait_recv()
        next_ahead.wait_send()
        last_out[...] = last_next[...]

    @pl.when(has_down)
    def _():
        below_out[...] = below_next[...]

    @pl.when(has_up)
    def _():
        above_out[...] = above_next[...]

    @pl.when(me == 0)
    def _():
        first_out[...] = jnp.zeros(first_out.shape, first_out.dtype)

    @pl.when(me == devices - 1)
    def _():
        last_out[...] = jnp.zeros(last_out.shape, last_out.dtype)

    @pl.when(g == 0)
    def _():
        below_out[...] = jnp.zeros(below_out.shape, below_out.dtype)

    @pl.when(g == groups - 1)
    def _():
        above_out[...] = jnp.zeros(above_out.shape, above_out.dtype)


def regrid(cross, sizes, ident, devices, tables, diffusion, fine, coarse, weights, flow):
    inner, stride, depth, hops, base_c, extra_c, step_c, inner_c, stride_c, hops_c = sizes
    planes, species, rows, depth_z = fine.shape
    part = devices // 2
    kept = jax.ShapeDtypeStruct(fine.shape, fine.dtype)
    plane = jax.ShapeDtypeStruct((1,) + fine.shape[1:], fine.dtype)
    edge = jax.ShapeDtypeStruct((species, planes, depth_z), fine.dtype)
    pool = devices * stride + (part - 1) * hops + planes // 2
    pool_c = (devices * stride_c + (part - 1) * hops_c) // 2
    vmem = pl.BlockSpec(memory_space=pltpu.VMEM)
    smem = pl.BlockSpec(memory_space=pltpu.SMEM)
    hbm = pl.BlockSpec(memory_space=pl.ANY)

    def held(count):
        return pltpu.VMEM((count,) + fine.shape[1:], fine.dtype)

    def held_c(count):
        return pltpu.VMEM((count, species, rows // 2, depth_z), fine.dtype)

    def sems(*shape):
        return [pltpu.SemaphoreType.DMA(shape)] * 2

    rim = pltpu.VMEM(edge.shape, edge.dtype)
    passed, passed_c = (part - 1) * hops, (part - 1) * hops_c // 2
    return pl.pallas_call(
        functools.partial(regrid_kernel, cross, sizes),
        out_shape=(kept, plane, plane, edge, edge),
        in_specs=[smem] * 2 + [hbm, hbm, vmem, hbm],
        out_specs=(hbm,) + (vmem,) * 4,
        scratch_shapes=[
            held(planes), pltpu.VMEM(coarse.shape, coarse.dtype), pltpu.VMEM(flow.shape, flow.dtype),
            held(planes), pltpu.SemaphoreType.DMA((3,)), pltpu.SemaphoreType.DMA((planes // 8,)),
            held(devices * stride), held_c(devices * stride_c // 2), held(pool), held_c(pool_c),
            held(devices * depth), held(passed), held_c(passed_c), held(passed), held_c(passed_c),
            held(planes + 2), rim, rim, rim, rim, rim, rim, rim, rim, held(1), held(1),
            *sems(3 * devices), *sems(2 * part), *sems(6), *sems(2, planes // 8),
        ],
        compiler_params=params(collective_id=ident, has_side_effects=True),
        name="regrid",
    )(tables, diffusion, fine, coarse, weights, flow)


def advance_kernel(steps, diffusion, u, before, after, first, last, below, above, flow, out):
    i = pl.program_id(0)
    block, species, rows, depth = u.shape
    row = lax.broadcasted_iota(jnp.int32, (rows, depth), 0)
    lane = lax.broadcasted_iota(jnp.int32, (rows, depth), 1)
    for x in range(block):
        coeffs = coefficients(flow, x)
        for s in range(species):
            if x > 0:
                lo = u[x - 1, s]
            else:
                lo = jnp.where(i == 0, first[0, s], before[0, s])
            if x < block - 1:
                hi = u[x + 1, s]
            else:
                hi = jnp.where(i == steps - 1, last[0, s], after[0, s])
            out[x, s] = update(
                diffusion[s], coeffs, u[x, s], lo, hi,
                below[s, pl.ds(x, 1), :], above[s, pl.ds(x, 1), :], row, lane,
            )


def advance(diffusion, u, first, last, below, above, flow):
    planes, species, rows, depth = u.shape
    block = 16 if planes % 16 == 0 else planes
    steps = planes // block
    edge_spec = pl.BlockSpec((species, block, depth), lambda i: (0, i, 0))
    plane_spec = pl.BlockSpec((1, species, rows, depth), lambda i: (0, 0, 0, 0))
    block_spec = pl.BlockSpec((block, species, rows, depth), lambda i: (i, 0, 0, 0))
    return pl.pallas_call(
        functools.partial(advance_kernel, steps),
        grid=(steps,),
        out_shape=jax.ShapeDtypeStruct(u.shape, u.dtype),
        in_specs=[
            pl.BlockSpec(memory_space=pltpu.SMEM),
            block_spec,
            pl.BlockSpec(
                (1, species, rows, depth), lambda i: (jnp.maximum(i * block - 1, 0), 0, 0, 0)
            ),
            pl.BlockSpec(
                (1, species, rows, depth),
                lambda i: (jnp.minimum(i * block + block, planes - 1), 0, 0, 0),
            ),
            plane_spec,
            plane_spec,
            edge_spec,
            edge_spec,
            pl.BlockSpec((block, 3, rows, depth), lambda i: (i, 0, 0, 0)),
        ],
        out_specs=block_spec,
        compiler_params=params(),
        name="advance",
    )(diffusion, u, u, u, first, last, below, above, flow)


def shift_up(value, axis):
    size = lax.axis_size(axis)
    return lax.ppermute(value, axis, [(i, i + 1) for i in range(size - 1)])


def shift_down(value, axis):
    size = lax.axis_size(axis)
    return lax.ppermute(value, axis, [(i + 1, i) for i in range(size - 1)])


def rims(u):
    rows = u.shape[2]
    below = shift_up(jnp.swapaxes(u[:, :, rows - 1], 0, 1), "grp")
    above = shift_down(jnp.swapaxes(u[:, :, 0], 0, 1), "grp")
    return shift_up(u[-1:], "dev"), shift_down(u[:1], "dev"), below, above


def on_device(old_fine, old_ids, old_coarse, coarse_ids, velocity, diffusion):
    devices = lax.axis_size("dev")
    group_count = lax.axis_size("grp")
    me = lax.axis_index("dev")
    planes = old_fine.shape[0]
    coarse_planes = old_coarse.shape[0]
    capacity = max(2, 2 * planes // devices)
    coarse_capacity = max(2, 2 * coarse_planes // devices)
    both = jnp.concatenate([old_ids[0], coarse_ids[0]])
    relaying = capacity >= 16 and devices % 2 == 0 and planes % 8 == 0 and group_count > 2
    if relaying:
        groups = gather_ids(both, group_count, devices)
    else:
        groups = lax.all_gather(both, ("grp", "dev")).reshape(group_count, devices, -1)
    weights = spread_weights(old_coarse.shape[3])

    def padded(fine, coarse):
        here = (jnp.arange(group_count) == lax.axis_index("grp"))[:, None, None]
        both_all = jnp.max(jnp.where(here, groups, -1), axis=0)
        own = jnp.max(jnp.where((jnp.arange(devices) == me)[:, None], both_all, -1), axis=0)
        coarse_send = send_table(own[planes:], coarse_planes, devices, coarse_capacity)
        coarse_table = receive_table(both_all[:, planes:], coarse_planes, coarse_capacity, me)
        coarse_out = pack_coarse(coarse_send, coarse)
        coarse_in = lax.all_to_all(coarse_out, "dev", split_axis=0, concat_axis=0, tiled=True)
        send = send_table(own[:planes], planes, devices, capacity)
        table = receive_table(both_all[:, :planes], planes, capacity, me)
        arrived = lax.all_to_all(pack_fine(send, fine), "dev", split_axis=0, concat_axis=0, tiled=True)
        interp = refine(coarse_table[None], coarse_in, weights)
        u = assemble(table, arrived, interp)
        u = advance(diffusion, u, *rims(u), velocity)
        return (u,) + rims(u)

    if relaying:
        choices = [capacity * k // 16 for k in CROSS]
        sizes = tuple(capacity * k // 16 for k in FINE) + tuple(coarse_capacity * k // 8 for k in COARSE)
        sizes = sizes[:5] + (1,) + sizes[5:]
        rows = group_count * devices
        flat = groups.reshape(rows, -1)
        place = jnp.stack([lax.axis_index("grp"), me]).astype(jnp.int32)
        tables = plan(
            place, flat[:, :planes], flat[:, planes:], group_count, devices, planes,
            coarse_planes, sizes, choices,
        )

        def relayed(count, ident, fine, coarse):
            return regrid(
                count, sizes, ident, devices, tables, diffusion, fine, coarse, weights, velocity
            )

        branches = [
            functools.partial(relayed, count, 1 + k) for k, count in enumerate(choices)
        ]
        state = lax.switch(tables[6, 0], branches + [padded], old_fine, old_coarse)
    else:
        state = padded(old_fine, old_coarse)
    return advance(diffusion, *state, velocity)


def solution(mesh):
    in_specs = (
        P("dev", None, "grp", None),
        P("grp", "dev"),
        P("dev", None, "grp", None),
        P("grp", "dev"),
        P("dev", None, "grp", None),
        P(),
    )
    out_specs = P("dev", None, "grp", None)
    return jax.shard_map(
        on_device, mesh=mesh, in_specs=in_specs, out_specs=out_specs, check_vma=False
    )
```

profile of v0, /device:TPU:1, one launch (start us, length us, event | category | flops | bytes accessed | tf_op | source)
XLA Modules:
  0.0 190.2 jit_solution(2756416699860223715)
XLA Ops:
  0.0 0.1 pad_add_fusion.place
  0.1 0.7 pad_add_fusion.1
  0.8 0.5 pad_bitcast_fusion.mine
  1.3 10.6 %gather_ids.1 = s32[32,1,128]{2,1,0:T(1,128)} custom-call(s32[1,128]{1,0:T(1,128)} %pad_bitcast_fusion.mine), custom_call_target="tpu_custom_call" | custom-call | tf_op jit(solution)/shard_map/gather_ids/pallas_call | solution.py:479
  12.0 0.7 fusion.7
  12.7 0.1 slice.62.coarse_ids
  12.8 4.5 %plan.1 = s32[8,128]{1,0:T(8,128)S(1)} custom-call(s32[2]{0:T(128)S(1)} %pad_add_fusion.place, s32[32,64]{1,0:T(8,128)S(1)} %bitcast.32, s32[32,32]{1,0:T(8,128)S(1)} %slice.62.coarse_ids), custom_call_target="tpu_custom_call" | custom-call | tf_op jit(solution)/shard_map/plan/pallas_call | solution.py:260
  17.3 0.5 slice.51
  18.6 163.5 %conditional.1 = ((f32[64,9,16,128]{3,2,1,0:T(8,128)}, f32[1,9,16,128]{3,2,1,0:T(8,128)}, f32[1,9,16,128]{3,2,1,0:T(8,128)}, f32[9,64,128]{2,1,0:T(8,128)}, f32[9,64,128]{2,1,0:T(8,128)})) conditional(s32[]{:T(128)} %bitcast.20, (s32[8,128]{1,0:T(8,128)S(1)}, f32[9]{0:T(128)}, f32[64,9,16,128]{3,2,1,0:T(8,128)}, ...), branch_computations={%region_0.1_spmd, %region_1.2_spmd, %region_2.3_spmd, %region_3.4_... | conditional | flops 40321056 | bytes 117691192 | solution.py:1092
  18.6 163.2 %regrid.6 = (f32[64,9,16,128]{3,2,1,0:T(8,128)}, f32[1,9,16,128]{3,2,1,0:T(8,128)}, f32[1,9,16,128]{3,2,1,0:T(8,128)}, f32[9,64,128]{2,1,0:T(8,128)}, f32[9,64,128]{2,1,0:T(8,128)}) custom-call(s32[8,128]{1,0:T(8,128)S(1)} %get-tuple-element.85.tables, f32[9]{0:T(128)} %get-tuple-element.86.diffusion, f32[64,9,16,128]{3,2,1,0:T(8,128)} %get-tuple-element.87.fine_hbm, ...), custom_call_target="tpu_custom_call" | custom-call | tf_op jit(solution)/shard_map/cond/branch_1_fun/regrid/pallas_call | solution.py:950
  182.1 8.1 %advance.3 = f32[64,9,16,128]{3,2,1,0:T(8,128)} custom-call(f32[9]{0:T(128)} %diffusion.1, f32[64,9,16,128]{3,2,1,0:T(8,128)} %get-tuple-element.121.u.before.after, f32[64,9,16,128]{3,2,1,0:T(8,128)} %get-tuple-element.121.u.before.after, f32[64,9,16,128]{3,2,1,0:T(8,128)} %get-tuple-element.121.u.before.after, f32[1,9,16,128]{3,2,1,0:T(8,128)} %get-tuple-element.122.first, ...), custom_call_target="tpu_custom_call" | custom-call | tf_op jit(solution)/shard_map/advance/pallas_call | solution.py:997
  (6 shorter events, 0.1 us)
where the time goes:
time: 188 us; the launch traced here: 190 us
  Pallas kernels  186 us (99%)
    pallas_call x1, Pallas kernels, regrid(): pl.pallas_call(functools.partial(regrid_kernel, cross, sizes), out_shape=...  163 us
    pallas_call x1, Pallas kernels, gather_ids(): pl.pallas_call(functools.partial(gather_kernel, groups, devices), out_sha...  10.6 us
    pallas_call x1, Pallas kernels, advance(): pl.pallas_call(functools.partial(advance_kernel, steps), grid=(steps,), o...  8.1 us
    pallas_call x1, Pallas kernels, plan(): pl.pallas_call(functools.partial(plan_kernel, groups, devices, block_len,...  4.54 us

commit v1 on v0

--- a/solution.py
+++ b/solution.py
@@ -7,7 +7,8 @@
 from jax.experimental.pallas import tpu as pltpu
 from jax.sharding import PartitionSpec as P
 
-CROSS = (34, 36, 38, 40, 44)
+CROSS = (32, 33, 34, 35, 36, 37, 38, 40, 44)
+LOOSE = 40
 FINE = (10, 11, 6, 6)
 COARSE = (4, 2, 6, 6, 4)
 VMEM_LIMIT = 48 * 1024 * 1024
@@ -125,9 +126,10 @@
     index = jnp.zeros(shape, jnp.float32)
     for i, m in enumerate(hops_at):
         index = index + m * (inside[i] + ahead[:, i : i + 1])
-    crowded = jnp.max(ahead + table, axis=(0, 1), keepdims=True) > hops
+    crowded = jnp.max(ahead + table, axis=(0, 1), keepdims=True) > float(hops)
     fault = jnp.max(as_float(bad), axis=(0, 1), keepdims=True) > 0.0
-    return via, spot, relayed, index.astype(jnp.int32), caps, crowded | fault
+    broken = jnp.where(crowded | fault, 1, 0)
+    return via, spot, relayed, index.astype(jnp.int32), caps, broken
 
 
 def widest_load(owner, devices):
@@ -139,7 +141,7 @@
 
 
 def plan_kernel(
-    groups, devices, block_len, coarse_len, sizes, choices,
+    groups, devices, block_len, coarse_len, sizes, choices, loose,
     place, fine_ids, coarse_ids, out, via_ref, where_ref, kind_ref, owner_ref, inner_ref,
 ):
     inner, stride, depth, hops, base_c, extra_c, step_c, inner_c, stride_c, hops_c = sizes
@@ -151,9 +153,7 @@
     width = out.shape[1]
     owner = jnp.where(fine >= 0, fine // block_len, -1)
     load = widest_load(owner, devices)
-    pick = sum(jnp.where(load > float(c), 1, 0) for c in choices)
-    wide = sum(jnp.where(pick == i, c, 0) for i, c in enumerate(choices))
-    base, extra = wide // part, lax.rem(wide, part)
+    pick = sum(jnp.where(load > float(c), 1, 0) for c in choices)[0, 0]
 
     both = jnp.where(fine >= 0, lax.rem(fine, block_len) // 2, -1)
     kind = lax.broadcasted_iota(jnp.int32, (devices, count), 0)
@@ -178,8 +178,8 @@
     needed = jnp.concatenate(needed, axis=0) < 1.5
     owner_c = jnp.where(needed, owner_c, -1)
 
-    def tables(owner, ids, length, stride, hops, depth, base, extra, step, inner, start):
-        via, spot, relayed, index, caps, fault = route(
+    def assign(owner, ids, length, stride, hops, depth, base, extra, step, inner):
+        via, spot, relayed, index, caps, broken = route(
             owner, devices, base, extra, step, inner, stride, depth, hops
         )
         n = owner.shape[1]
@@ -192,15 +192,18 @@
         flat = jnp.where(
             early, devices * late + block * depth + spot - (cap - depth), block * late + spot
         )
-        flat = jnp.where(via >= 0, flat, -1)
-        arrivals = devices * stride
-        small = max(n, arrivals + (part - 1) * hops + 1) <= 256
-        exact = None if small else lax.Precision.HIGHEST
         via_ref[:, 0:n] = jnp.where(relayed, via, -1)
-        where_ref[:, 0:n] = flat
+        where_ref[:, 0:n] = jnp.where(via >= 0, flat, -1)
         kind_ref[:, 0:n] = index
         owner_ref[:, 0:n] = owner
         inner_ref[:, 0:n] = ids - me * length
+        return broken
+
+    def tables(n, stride, hops, start):
+        arrivals = devices * stride
+        passed = (part - 1) * hops
+        small = max(n, arrivals + passed + 1) <= 256
+        exact = None if small else lax.Precision.HIGHEST
         mine = pl.ds(pl.multiple_of(g * devices, devices), devices)
         via_g = via_ref[mine, 0:n]
         flat_g = where_ref[mine, 0:n]
@@ -212,9 +215,10 @@
         slots = lax.broadcasted_iota(jnp.int32, (width, n), 0)
         place_at = lax.broadcasted_iota(jnp.int32, (devices, n), 1).astype(jnp.float32)
         send = same_dim(place_at, as_float(own == slots), exact)
-        lane = lax.rem(owner_g + 2 * part - lax.rem(me, part), part) - 1
+        seat = lax.rem(me, part)
+        lane = lax.rem(owner_g + 2 * part - seat, part) - 1
         handed = jnp.where(via_g == me, lane * hops + index_g, -1)
-        back = lax.rem(lax.rem(me, part) + part - lax.rem(jnp.maximum(via_g, 0), part), part) - 1
+        back = lax.rem(seat + part - lax.rem(jnp.maximum(via_g, 0), part), part) - 1
         spot_at = jnp.where(via_g >= 0, arrivals + back * hops + index_g, flat_g)
         inside = jnp.where(owner_g == me, inner_g, -1)
         flat_f = flat_g.astype(jnp.float32)
@@ -234,32 +238,43 @@
         whole = (final + 0.5).astype(jnp.int32)
         missing = start + (at // 2 if start else 0)
         whole = jnp.where(whole > 0, whole - 1, missing)
-        send = (send + 0.5).astype(jnp.int32)
-        relay = (relay + 0.5).astype(jnp.int32)
-        return send, relay, whole, fault
-
+        return [(send + 0.5).astype(jnp.int32), (relay + 0.5).astype(jnp.int32), whole]
+
+    broken_c = assign(
+        owner_c, coarse, coarse_len, stride_c, hops_c, stride_c, base_c, extra_c, step_c, inner_c,
+    )
+    parts_c = tables(count_c, stride_c, hops_c, 0)
+
+    def attempt(carry):
+        pick, _ = carry
+        wide = sum(jnp.where(pick == i, c, 0) for i, c in enumerate(choices))
+        broken = assign(
+            owner, fine, block_len, stride, hops, depth, wide // part, lax.rem(wide, part), 1,
+            inner + jnp.where(wide >= loose, 1, 0),
+        )
+        return pick + 1, broken[0, 0]
+
+    def again(carry):
+        return (carry[1] > 0) & (carry[0] < len(choices))
+
+    after, broken = lax.while_loop(again, attempt, (pick, jnp.int32(1)))
     fill = devices * stride + (part - 1) * hops
-    send, relay, final, fault = tables(
-        owner, fine, block_len, stride, hops, depth, base, extra, 1, inner, fill
-    )
-    send_c, relay_c, final_c, fault_c = tables(
-        owner_c, coarse, coarse_len, stride_c, hops_c, stride_c, base_c, extra_c, step_c, inner_c, 0
-    )
-    pick = jnp.where(fault | fault_c, len(choices), pick)
-    parts = (send, relay, final, send_c, relay_c, final_c)
+    parts = tables(count, stride, hops, fill)
+    pick = jnp.where((broken > 0) | (broken_c[0, 0] > 0), len(choices), after - 1)
+    parts = parts + parts_c
     for i, value in enumerate(parts):
         out[i : i + 1] = value[0:1]
-    out[len(parts) : len(parts) + 1] = jnp.broadcast_to(pick, (1, width)).astype(jnp.int32)
-
-
-def plan(place, fine_ids, coarse_ids, groups, devices, block_len, coarse_len, sizes, choices):
+    out[len(parts) : len(parts) + 1] = jnp.zeros((1, width), jnp.int32) + pick
+
+
+def plan(place, fine_ids, coarse_ids, groups, devices, block_len, coarse_len, sizes, choices, loose):
     rows, count = fine_ids.shape
     longest = max(devices * sizes[1], devices * sizes[8], count, (devices // 2) * max(sizes[3], sizes[9]))
     width = -(-longest // 128) * 128
     cells = pltpu.VMEM((rows, max(count, coarse_ids.shape[1])), jnp.int32)
     return pl.pallas_call(
         functools.partial(
-            plan_kernel, groups, devices, block_len, coarse_len, sizes, choices
+            plan_kernel, groups, devices, block_len, coarse_len, sizes, choices, loose
         ),
         out_shape=jax.ShapeDtypeStruct((8, width), jnp.int32),
         in_specs=[
@@ -1078,12 +1093,12 @@
         place = jnp.stack([lax.axis_index("grp"), me]).astype(jnp.int32)
         tables = plan(
             place, flat[:, :planes], flat[:, planes:], group_count, devices, planes,
-            coarse_planes, sizes, choices,
+            coarse_planes, sizes, choices, capacity * LOOSE // 16,
         )
 
         def relayed(count, ident, fine, coarse):
             return regrid(
-                count, sizes, ident, devices, tables, diffusion, fine, coarse, weights, velocity
+                count, (sizes[0] + (count >= capacity * LOOSE // 16),) + sizes[1:], ident, devices, tables, diffusion, fine, coarse, weights, velocity
             )
 
         branches = [

time: 188 us -> 184 us (0.979)
  Pallas kernels: 186 us -> 181 us
    pallas_call x1, Pallas kernels: 163 us -> 158 us  [regrid(): pl.pallas_call(functools.partial(regrid_kernel, cross, sizes), out_shape=...]
where the time goes in v1:
time: 184 us; the launch traced here: 185 us
  Pallas kernels  181 us (98%)
  local copies, waits for them, and re-layouts  1.85 us (1%)
    pallas_call x1, Pallas kernels, regrid(): pl.pallas_call(functools.partial(regrid_kernel, cross, sizes), out_shape=...  158 us
    pallas_call x1, Pallas kernels, gather_ids(): pl.pallas_call(functools.partial(gather_kernel, groups, devices), out_sha...  10.6 us
    pallas_call x1, Pallas kernels, advance(): pl.pallas_call(functools.partial(advance_kernel, steps), grid=(steps,), o...  8.1 us
    pallas_call x1, Pallas kernels, plan(): pl.pallas_call(functools.partial(plan_kernel, groups, devices, block_len,...  5 us

profile of v1, /device:TPU:1, one launch (start us, length us, event | category | flops | bytes accessed | tf_op | source)
XLA Modules:
  0.0 185.2 jit_solution(190431142057891750)
XLA Ops:
  0.0 0.1 pad_add_fusion.place
  0.1 0.7 pad_add_fusion.1
  0.8 0.5 pad_bitcast_fusion.mine
  1.3 10.6 %gather_ids.1 = s32[32,1,128]{2,1,0:T(1,128)} custom-call(s32[1,128]{1,0:T(1,128)} %pad_bitcast_fusion.mine), custom_call_target="tpu_custom_call" | custom-call | tf_op jit(solution)/shard_map/gather_ids/pallas_call | solution.py:494
  12.0 0.7 fusion.7
  12.7 0.1 slice.62.coarse_ids
  12.8 5.0 %plan.1 = s32[8,128]{1,0:T(8,128)S(1)} custom-call(s32[2]{0:T(128)S(1)} %pad_add_fusion.place, s32[32,64]{1,0:T(8,128)S(1)} %bitcast.32, s32[32,32]{1,0:T(8,128)S(1)} %slice.62.coarse_ids), custom_call_target="tpu_custom_call" | custom-call | tf_op jit(solution)/shard_map/plan/pallas_call | solution.py:275
  17.8 0.5 slice.51
  19.1 158.0 %conditional.1 = ((f32[64,9,16,128]{3,2,1,0:T(8,128)}, f32[1,9,16,128]{3,2,1,0:T(8,128)}, f32[1,9,16,128]{3,2,1,0:T(8,128)}, f32[9,64,128]{2,1,0:T(8,128)}, f32[9,64,128]{2,1,0:T(8,128)})) conditional(s32[]{:T(128)} %bitcast.20, (s32[8,128]{1,0:T(8,128)S(1)}, f32[9]{0:T(128)}, f32[64,9,16,128]{3,2,1,0:T(8,128)}, ...), branch_computations={%region_0.1_spmd, %region_1.2_spmd, %region_2.3_spmd, %region_3.4_... | conditional | flops 40321056 | bytes 117691192 | solution.py:1107
  19.1 157.7 %regrid.11 = (f32[64,9,16,128]{3,2,1,0:T(8,128)}, f32[1,9,16,128]{3,2,1,0:T(8,128)}, f32[1,9,16,128]{3,2,1,0:T(8,128)}, f32[9,64,128]{2,1,0:T(8,128)}, f32[9,64,128]{2,1,0:T(8,128)}) custom-call(s32[8,128]{1,0:T(8,128)S(1)} %get-tuple-element.139.tables, f32[9]{0:T(128)} %get-tuple-element.140.diffusion, f32[64,9,16,128]{3,2,1,0:T(8,128)} %get-tuple-element.141.fine_hbm, ...), custom_call_target="tpu_custom_call" | custom-call | tf_op jit(solution)/shard_map/cond/branch_2_fun/regrid/pallas_call | solution.py:965
  177.1 8.1 %advance.3 = f32[64,9,16,128]{3,2,1,0:T(8,128)} custom-call(f32[9]{0:T(128)} %diffusion.1, f32[64,9,16,128]{3,2,1,0:T(8,128)} %get-tuple-element.193.u.before.after, f32[64,9,16,128]{3,2,1,0:T(8,128)} %get-tuple-element.193.u.before.after, f32[64,9,16,128]{3,2,1,0:T(8,128)} %get-tuple-element.193.u.before.after, f32[1,9,16,128]{3,2,1,0:T(8,128)} %get-tuple-element.194.first, ...), custom_call_target="tpu_custom_call" | custom-call | tf_op jit(solution)/shard_map/advance/pallas_call | solution.py:1012
  (6 shorter events, 0.1 us)

commit v2 on v1

--- a/solution.py
+++ b/solution.py
@@ -2,6 +2,7 @@
 
 import jax
 import jax.numpy as jnp
+import numpy as np
 from jax import lax
 from jax.experimental import pallas as pl
 from jax.experimental.pallas import tpu as pltpu
@@ -373,14 +374,14 @@
 
 def spread_weights(half):
     depth = 2 * half
-    coarse = jnp.arange(half)[:, None]
-    fine = jnp.arange(depth)[None, :]
-    centre = (fine // 2 == coarse).astype(jnp.float32)
-    up = (jnp.minimum(fine // 2 + 1, half - 1) == coarse).astype(jnp.float32)
-    down = (jnp.maximum(fine // 2 - 1, 0) == coarse).astype(jnp.float32)
-    side = jnp.where(fine % 2 == 1, 0.125, -0.125)
-    both = jnp.concatenate([centre, centre + side * (up - down)], axis=1)
-    return jnp.concatenate([both, both], axis=0)
+    coarse = np.arange(half)[:, None]
+    fine = np.arange(depth)[None, :]
+    centre = (fine // 2 == coarse).astype(np.float32)
+    up = (np.minimum(fine // 2 + 1, half - 1) == coarse).astype(np.float32)
+    down = (np.maximum(fine // 2 - 1, 0) == coarse).astype(np.float32)
+    side = np.where(fine % 2 == 1, 0.125, -0.125).astype(np.float32)
+    both = np.concatenate([centre, centre + side * (up - down)], axis=1)
+    return np.concatenate([both, both], axis=0)
 
 
 def refine(table, pairs, weights):
@@ -724,17 +725,6 @@
 
     lax.fori_loop(0, passed, keep_passed, 0)
 
-    def assemble(p, carry):
-        at = tables[2, p]
-        for s in range(species):
-            value = pool[at, s]
-            state[p + 1, s] = value
-            low[s, pl.ds(p, 1), :] = value[0:1]
-            high[s, pl.ds(p, 1), :] = value[rows - 1 : rows]
-        return carry
-
-    lax.fori_loop(0, planes, assemble, 0)
-
     def edge_copy(source, target, at, to):
         return pltpu.make_async_remote_copy(
             src_ref=source,
@@ -760,27 +750,45 @@
     down, up = {"grp": g - 1}, {"grp": g + 1}
     ahead = edge_copy(state.at[pl.ds(planes, 1)], state.at[pl.ds(0, 1)], 0, right)
     back = edge_copy(state.at[pl.ds(1, 1)], state.at[pl.ds(planes + 1, 1)], 1, left)
-    rise = edge_copy(high, below, 2, up)
-    sink = edge_copy(low, above, 3, down)
     has_left, has_right = me > 0, me < devices - 1
     has_down, has_up = g > 0, g < groups - 1
 
-    @pl.when(has_up)
-    def _():
-        rise.start()
-
-    @pl.when(has_down)
-    def _():
-        sink.start()
-
-    @pl.when(has_right)
-    def _():
-        ahead.start()
-
-    @pl.when(has_left)
-    def _():
-        back.start()
-
+    blocks = planes // 8
+
+    def assemble_block(turn, carry):
+        b = lax.rem(turn + blocks - 1, blocks)
+
+        def assemble(k, carry):
+            p = b * 8 + k
+            at = tables[2, p]
+            for s in range(species):
+                value = pool[at, s]
+                state[p + 1, s] = value
+                low[s, pl.ds(p, 1), :] = value[0:1]
+                high[s, pl.ds(p, 1), :] = value[rows - 1 : rows]
+            return carry
+
+        lax.fori_loop(0, 8, assemble, 0)
+
+        @pl.when((turn == 0) & has_right)
+        def _():
+            ahead.start()
+
+        @pl.when((turn == 1) & has_left)
+        def _():
+            back.start()
+
+        @pl.when(has_up)
+        def _():
+            row_copy(high, below, b, 2, up).start()
+
+        @pl.when(has_down)
+        def _():
+            row_copy(low, above, b, 3, down).start()
+
+        return carry
+
+    lax.fori_loop(0, blocks, assemble_block, 0)
     for move in coarse_moves + relays_c + early_moves + late_moves + relays:
         move.wait_send()
 
@@ -792,14 +800,6 @@
     def _():
         back.wait_recv()
 
-    @pl.when(has_down)
-    def _():
-        rise.wait_recv()
-
-    @pl.when(has_up)
-    def _():
-        sink.wait_recv()
-
     @pl.when(has_right)
     def _():
         ahead.wait_send()
@@ -807,14 +807,6 @@
     @pl.when(has_left)
     def _():
         back.wait_send()
-
-    @pl.when(has_up)
-    def _():
-        rise.wait_send()
-
-    @pl.when(has_down)
-    def _():
-        sink.wait_send()
 
     @pl.when(me == 0)
     def _():
@@ -839,7 +831,6 @@
     loads[2].wait()
     next_ahead = edge_copy(out.at[pl.ds(planes - 1, 1)], first_next, 4, right)
     next_back = edge_copy(out.at[pl.ds(0, 1)], last_next, 5, left)
-    blocks = planes // 8
 
     def save(b):
         cut = pl.ds(b * 8, 8)
@@ -847,6 +838,14 @@
 
     def advance_block(turn, carry):
         b = lax.rem(turn + blocks - 1, blocks)
+
+        @pl.when(has_down)
+        def _():
+            row_copy(high, below, b, 2, up).wait_recv()
+
+        @pl.when(has_up)
+        def _():
+            row_copy(low, above, b, 3, down).wait_recv()
 
         def advance_plane(k, carry):
             p = b * 8 + k
@@ -891,11 +890,13 @@
         def _():
             row_copy(high_next, below_next, b, 0, up).wait_recv()
             row_copy(low_next, above_next, b, 1, down).wait_send()
+            row_copy(low, above, b, 3, down).wait_send()
 
         @pl.when(has_up)
         def _():
             row_copy(low_next, above_next, b, 1, down).wait_recv()
             row_copy(high_next, below_next, b, 0, up).wait_send()
+            row_copy(high, below, b, 2, up).wait_send()
 
         return carry
 
@@ -973,7 +974,7 @@
             held(devices * stride), held_c(devices * stride_c // 2), held(pool), held_c(pool_c),
             held(devices * depth), held(passed), held_c(passed_c), held(passed), held_c(passed_c),
             held(planes + 2), rim, rim, rim, rim, rim, rim, rim, rim, held(1), held(1),
-            *sems(3 * devices), *sems(2 * part), *sems(6), *sems(2, planes // 8),
+            *sems(3 * devices), *sems(2 * part), *sems(6), *sems(4, planes // 8),
         ],
         compiler_params=params(collective_id=ident, has_side_effects=True),
         name="regrid",
@@ -1066,7 +1067,7 @@
         groups = gather_ids(both, group_count, devices)
     else:
         groups = lax.all_gather(both, ("grp", "dev")).reshape(group_count, devices, -1)
-    weights = spread_weights(old_coarse.shape[3])
+    weights = jnp.asarray(spread_weights(old_coarse.shape[3]))
 
     def padded(fine, coarse):
         here = (jnp.arange(group_count) == lax.axis_index("grp"))[:, None, None]

time: 184 us -> 187 us (1.016); the launches traced: 185 us -> 185 us
  no operation moved by 1% of the time
where the time goes in v2:
time: 187 us; the launch traced here: 185 us
  Pallas kernels  181 us (97%)
    pallas_call x1, Pallas kernels, regrid(): pl.pallas_call(functools.partial(regrid_kernel, cross, sizes), out_shape=...  157 us
    pallas_call x1, Pallas kernels, gather_ids(): pl.pallas_call(functools.partial(gather_kernel, groups, devices), out_sha...  10.6 us
    pallas_call x1, Pallas kernels, advance(): pl.pallas_call(functools.partial(advance_kernel, steps), grid=(steps,), o...  8.1 us
    pallas_call x1, Pallas kernels, plan(): pl.pallas_call(functools.partial(plan_kernel, groups, devices, block_len,...  5 us

profile of v2, /device:TPU:1, one launch (start us, length us, event | category | flops | bytes accessed | tf_op | source)
XLA Modules:
  0.0 184.7 jit_solution(10237310662724727412)
XLA Ops:
  0.0 0.1 pad_add_fusion.place
  0.1 0.7 pad_add_fusion.1
  0.8 0.5 pad_bitcast_fusion.mine
  1.3 10.6 %gather_ids.1 = s32[32,1,128]{2,1,0:T(1,128)} custom-call(s32[1,128]{1,0:T(1,128)} %pad_bitcast_fusion.mine), custom_call_target="tpu_custom_call" | custom-call | tf_op jit(solution)/shard_map/gather_ids/pallas_call | solution.py:495
  12.0 0.7 fusion.6
  12.7 0.1 slice.62.coarse_ids
  12.8 5.0 %plan.1 = s32[8,128]{1,0:T(8,128)S(1)} custom-call(s32[2]{0:T(128)S(1)} %pad_add_fusion.place, s32[32,64]{1,0:T(8,128)S(1)} %bitcast.32, s32[32,32]{1,0:T(8,128)S(1)} %slice.62.coarse_ids), custom_call_target="tpu_custom_call" | custom-call | tf_op jit(solution)/shard_map/plan/pallas_call | solution.py:276
  17.8 0.5 slice.51
  19.0 157.7 %conditional.1 = ((f32[64,9,16,128]{3,2,1,0:T(8,128)}, f32[1,9,16,128]{3,2,1,0:T(8,128)}, f32[1,9,16,128]{3,2,1,0:T(8,128)}, f32[9,64,128]{2,1,0:T(8,128)}, f32[9,64,128]{2,1,0:T(8,128)})) conditional(s32[]{:T(128)} %bitcast.20, (s32[8,128]{1,0:T(8,128)S(1)}, f32[9]{0:T(128)}, f32[64,9,16,128]{3,2,1,0:T(8,128)}, ...), branch_computations={%region_0.1_spmd, %region_1.2_spmd, %region_2.3_spmd, %region_3.4_... | conditional | flops 40321056 | bytes 117166872 | solution.py:1108
  19.0 157.4 %regrid.11 = (f32[64,9,16,128]{3,2,1,0:T(8,128)}, f32[1,9,16,128]{3,2,1,0:T(8,128)}, f32[1,9,16,128]{3,2,1,0:T(8,128)}, f32[9,64,128]{2,1,0:T(8,128)}, f32[9,64,128]{2,1,0:T(8,128)}) custom-call(s32[8,128]{1,0:T(8,128)S(1)} %get-tuple-element.139.tables, f32[9]{0:T(128)} %get-tuple-element.140.diffusion, f32[64,9,16,128]{3,2,1,0:T(8,128)} %get-tuple-element.141.fine_hbm, ...), custom_call_target="tpu_custom_call" | custom-call | tf_op jit(solution)/shard_map/cond/branch_2_fun/regrid/pallas_call | solution.py:966
  176.6 8.1 %advance.3 = f32[64,9,16,128]{3,2,1,0:T(8,128)} custom-call(f32[9]{0:T(128)} %diffusion.1, f32[64,9,16,128]{3,2,1,0:T(8,128)} %get-tuple-element.193.u.before.after, f32[64,9,16,128]{3,2,1,0:T(8,128)} %get-tuple-element.193.u.before.after, f32[64,9,16,128]{3,2,1,0:T(8,128)} %get-tuple-element.193.u.before.after, f32[1,9,16,128]{3,2,1,0:T(8,128)} %get-tuple-element.194.first, ...), custom_call_target="tpu_custom_call" | custom-call | tf_op jit(solution)/shard_map/advance/pallas_call | solution.py:1013
